TPU v7x, 128 devices: a whole 4x4x4 slice. The times are simulated.
128 devices in a mesh: gx: 8 (over x, z_hi), gy: 16 (over y, z_lo, core).
Axes of the slice: x: 4, y: 4, z: 4 (z_hi: 2, z_lo: 2; z = z_hi * 2 + z_lo), core: 2. Of those that a mesh axis runs over, the one named last changes fastest.
Arguments:
- traveltime: float32 [8, 32, 128, 1024], P(None, None, 'gy', 'gx'), may hold values from 1 to 4
- adjoint_start: float32 [8, 32, 128, 1024], P(None, None, 'gy', 'gx'), may hold values from -6 to 6
- upwind_flags: int32 [8, 32, 128, 1024], P(None, None, 'gy', 'gx'), may hold values from 0 to 7, as said below
- slowness: float32 [32, 128, 1024], P(None, 'gy', 'gx'), may hold values from 0.15 to 0.6
- residual_rows: float32 [32768, 8], P(('gx', 'gy')), may hold values from -6 to 6
- station_tile: int32 [32768, 1], P(('gx', 'gy')), may hold values from 0 to 127; in each aligned block of 256 rows (0 to 255, 256 to 511, ...) at most 4 rows name the same one
- station_cell: int32 [32768], P(('gx', 'gy')), may hold values from 0 to 32767
Outputs:
- adjoint: float32 [8, 32, 128, 1024], P(None, None, 'gy', 'gx')
- gradient: float32 [32, 128, 1024], P(None, 'gy', 'gx')
Inputs may be any that keep to these rules, and one draw needn't show every extreme that they name: `upwind_flags`: bit k of a cell's value is 1 where its upwind neighbour along x, y, z (k = 0, 1, 2) lies at the higher index; at every face of the grid the upwind neighbour lies inside the grid. `station_tile`: among the records of one device no tile is named more than 4 times, a bound that some block reaches.
All inputs are finite; a program needn't handle non-finite values.
Results may differ from a plain program's by a relative error of at most 0.00002.
Values sent between devices are 32-bit elements; how exact they have to be, the bound alone decides.
No kernel may reach another device: no remote copies, remote signals or barrier semaphores. Data moves between devices by JAX's collectives and lax.ppermute only.
A program may use at most 128 MiB of HBM per device.

v0:
```python
import jax
import jax.numpy as jnp
from jax import lax
from jax.experimental import pallas as pl
from jax.experimental.pallas import tpu as pltpu
from jax.sharding import PartitionSpec as P

F32 = jnp.float32
BF16 = jnp.bfloat16
I32 = jnp.int32

SRC = 8
Z = 32
TY = 8
TX = 128
PLANES = SRC + 1
ROWS = Z * TY
HALO = 4
CAP = 4
GROUP = 40
PAD = 8
NEAR = tuple((dx, dy) for dx in (-1, 0, 1) for dy in (-1, 0, 1))

NT = (((1,), (1,)), ((), ()))
NN = (((1,), (0,)), ((), ()))


def iota(shape, dim):
    return lax.broadcasted_iota(I32, shape, dim)


def turn(v, by):
    return pltpu.roll(v, by % TX, 1)


def level(z):
    return pl.ds(pl.multiple_of(z * TY, TY), TY)


def dot(a, b, dims=NT):
    return lax.dot_general(a, b, dims, preferred_element_type=F32)


def split3(v):
    hi = v.astype(BF16).astype(F32)
    rest = v - hi
    mid = rest.astype(BF16).astype(F32)
    return hi, mid, rest - mid


def is_even(axis):
    return lax.rem(lax.axis_index(axis), 2) == 0


def records_kernel(rows_ref, tile_ref, cell_ref, out_ref, parts, shifted):
    count = rows_ref.shape[1]
    devices = out_ref.shape[0]
    tile = tile_ref[...]
    named = (iota((devices, count), 0) == tile).astype(F32)
    earlier = (iota((count, count), 0) < iota((count, count), 1)).astype(F32).astype(BF16)
    picks = named.astype(BF16)
    before = dot(picks, earlier, NN)
    rank = jnp.sum(before * named, axis=0, keepdims=True).astype(I32)
    values = rows_ref[...]
    cells = (cell_ref[...] + 1).astype(F32)
    blocks = [jnp.where(rank == k, values, 0.0) for k in range(CAP)]
    blocks.append(jnp.where(rank == iota((8, count), 0), cells, 0.0))
    for k, block in enumerate(blocks):
        for n, part in enumerate(split3(block)):
            parts[n, 8 * k : 8 * k + 8, :] = part
    own = sum(dot(picks, parts[n].astype(BF16)) for n in range(3))
    shifted[...] = jnp.zeros(shifted.shape, F32)
    shifted[32 : 32 + devices, 0:GROUP] = own
    lane = iota((devices, TX), 1)
    ty = lax.rem(iota((devices, TX), 0), 16)
    for c in range(3):
        chunk = jnp.zeros((devices, TX), F32)
        for i in range(3):
            dx, dy = NEAR[3 * c + i]
            off = 32 + 16 * dx + dy
            theirs = shifted[off : off + devices, :]
            held = (lane >= GROUP * i) & (lane < GROUP * (i + 1))
            if dy:
                held = held & (ty + dy >= 0) & (ty + dy < 16)
            chunk = jnp.where(held, turn(theirs, GROUP * i) if i else theirs, chunk)
        out_ref[:, c * TX : (c + 1) * TX] = chunk


def edges_kernel(t_ref, a_ref, f_ref, first_ref, second_ref, own_ref):
    even = is_even("gx")
    lane = iota((TY, TX), 1)
    j = lane & 7

    def at_level(z, carry):
        here = level(z)
        packed = []
        for n, ref in enumerate((t_ref, a_ref, f_ref)):
            both = None
            for s in range(SRC):
                v = turn(ref[s, here, :].astype(F32), HALO + 8 * s)
                both = v if both is None else jnp.where(lane >> 3 == s, v, both)
            own_ref[n, here, :] = both
            packed.append(both)
        t, a, f = packed
        f = turn(f, 64)
        to_right = jnp.where(lane < 64, jnp.where(j < 4, t, turn(a, 4)), f)
        to_left = jnp.where(lane < 64, jnp.where(j < 4, turn(t, -4), a), f)
        first_ref[here, :] = jnp.where(even, to_right, to_left)
        second_ref[here, :] = jnp.where(even, to_left, to_right)
        return carry

    lax.fori_loop(0, Z, at_level, 0, unroll=2)


def strips_kernel(
    t_ref, a_ref, f_ref, own_ref, x0_ref, x1_ref, strip_ref, first_ref, second_ref
):
    even = is_even("gx")
    lane = iota((TY, TX), 1)
    j = lane & 7
    near = j < 4

    def at_level(z, carry):
        here = level(z)
        x0, x1 = x0_ref[here, :], x1_ref[here, :]
        left = jnp.where(even, x1, x0)
        right = jnp.where(even, x0, x1)
        t, a, f = own_ref[0, here, :], own_ref[1, here, :], own_ref[2, here, :]
        strip_ref[0, here, :] = jnp.where(
            lane < 64,
            jnp.where(near, left, t),
            turn(jnp.where(near, t, turn(right, 4)), 64),
        )
        strip_ref[1, here, :] = jnp.where(
            lane < 64,
            jnp.where(near, turn(left, -4), a),
            turn(jnp.where(near, a, right), 64),
        )
        strip_ref[2, here, :] = jnp.where(
            lane < 64,
            jnp.where(near, turn(left, 64), f),
            jnp.where(near, turn(f, 64), right),
        )
        return carry

    lax.fori_loop(0, Z, at_level, 0, unroll=2)

    def pack(out, high):
        edge = pl.ds(TY - 1 if high else 0, Z, stride=TY)
        inner = pl.ds(TY - 2 if high else 1, Z, stride=TY)
        for p in range(PLANES):
            if p < SRC:
                t, a, f = t_ref.at[p], a_ref.at[p], f_ref.at[p]
            else:
                t, a, f = strip_ref.at[0], strip_ref.at[1], strip_ref.at[2]
            out[0, p] = t[edge, :]
            out[1, p] = f[edge, :].astype(F32)
            out[2, p] = a[edge, :]
            out[3, p] = t[inner, :]
            up = (f[inner, :].astype(I32) & 2) != 0
            given = a[inner, :]
            out[4, p] = jnp.where(up, given, 0.0) if high else jnp.where(up, 0.0, given)

    even_y = is_even("gy")

    @pl.when(even_y)
    def _():
        pack(first_ref, True)
        pack(second_ref, False)

    @pl.when(jnp.logical_not(even_y))
    def _():
        pack(first_ref, False)
        pack(second_ref, True)


def both_sides(strip, j):
    return jnp.where(j == 3, strip, turn(strip, 62))


def beside(v, patch, lane):
    if patch is None:
        return turn(v, 1), turn(v, -1)
    return jnp.where(lane == 0, patch, turn(v, 1)), jnp.where(lane == TX - 1, patch, turn(v, -1))


def patch_of(sides, p):
    return None if p == SRC else turn(sides, -(8 * p + 3))


def given_low(flag, bit, theirs, mine):
    return jnp.where((flag & bit) != 0, jnp.maximum(theirs - mine, 0.0), 0.0)


def given_high(flag, bit, theirs, mine):
    return jnp.where((flag & bit) == 0, jnp.maximum(theirs - mine, 0.0), 0.0)


def coef(flag, bit, low, high, mine):
    return jnp.maximum(mine - jnp.where((flag & bit) != 0, high, low), 0.0)


def coefficients_kernel(
    t_ref, a_ref, f_ref, strip_ref, y0_ref, y1_ref, g_ref, rden_ref, x_ref, edge_ref, row_ref, rows
):
    even_y = is_even("gy")
    blank = jnp.zeros((PAD, TX), F32)
    for k in range(5):
        for p in range(PLANES):
            first, second = y0_ref[k, p], y1_ref[k, p]
            rows[0, k, p, PAD : PAD + Z, :] = jnp.where(even_y, second, first)
            rows[1, k, p, PAD : PAD + Z, :] = jnp.where(even_y, first, second)
            if k < 3:
                for side in range(2):
                    rows[side, k, p, 0:PAD, :] = blank
                    rows[side, k, p, PAD + Z : PAD + Z + PAD, :] = blank

    lane = iota((TY, TX), 1)
    j = lane & 7
    row = iota((TY, TX), 0)

    def refs(p):
        if p < SRC:
            return t_ref.at[p], a_ref.at[p], f_ref.at[p]
        return strip_ref.at[0], strip_ref.at[1], strip_ref.at[2]

    def at_level(z, carry):
        here = level(z)
        below = level(jnp.maximum(z - 1, 0))
        above = level(jnp.minimum(z + 1, Z - 1))
        sides = [both_sides(strip_ref[n, here, :], j) for n in range(3)]

        def halo(side, k, p):
            return jnp.broadcast_to(rows[side, k, p, pl.ds(PAD + z, 1), :], (TY, TX))

        def down(v, h):
            return jnp.where(row == 0, h, pltpu.roll(v, 1, 0))

        def up(v, h):
            return jnp.where(row == TY - 1, h, pltpu.roll(v, TY - 1, 0))

        for p in range(PLANES):
            t_p, a_p, f_p = refs(p)
            t = t_p[here, :]
            f = f_p[here, :].astype(F32)
            a = a_p[here, :]
            tl, tr = beside(t, patch_of(sides[0], p), lane)
            al, ar = beside(a, patch_of(sides[1], p), lane)
            fl, fr = beside(f, patch_of(sides[2], p), lane)
            tu, td = down(t, halo(0, 0, p)), up(t, halo(1, 0, p))
            fu, fd = down(f, halo(0, 1, p)), up(f, halo(1, 1, p))
            au, ad = down(a, halo(0, 2, p)), up(a, halo(1, 2, p))
            tm = jnp.where(z > 0, t_p[below, :], 0.0)
            tp = jnp.where(z < Z - 1, t_p[above, :], 0.0)
            f = f.astype(I32)
            den = 1.0 + coef(f, 1, tl, tr, t) + coef(f, 2, tu, td, t) + coef(f, 4, tm, tp, t)
            rden = 1.0 / den
            shares = [
                given_low(fl.astype(I32), 1, tl, t),
                given_high(fr.astype(I32), 1, tr, t),
                given_low(fu.astype(I32), 2, tu, t),
                given_high(fd.astype(I32), 2, td, t),
                given_low(f_p[below, :].astype(I32), 4, tm, t),
                given_high(f_p[above, :].astype(I32), 4, tp, t),
            ]
            shares = [g * rden for g in shares]
            total = None
            for k, (g, v) in enumerate(zip(shares, (al, ar, au, ad, a_p[below, :], a_p[above, :]))):
                g_ref[k, p, here, :] = g
                total = g * v if total is None else total + g * v
            rden_ref[p, here, :] = rden
            x_ref[p, here, :] = total
        return carry

    lax.fori_loop(0, Z, at_level, 0)

    lane = iota((Z, TX), 1)
    j = lane & 7
    for side in range(2):
        edge = pl.ds(0 if side == 0 else TY - 1, Z, stride=TY)
        sides = [both_sides(rows[side, n, SRC, PAD : PAD + Z, :], j) for n in range(3)]
        for p in range(PLANES):
            t_p, a_p, f_p = refs(p)
            edge_ref[side, p] = g_ref[2 + side, p, edge, :]

            def at(k, shift=0):
                return rows[side, k, p, PAD + shift : PAD + shift + Z, :]

            t, f, a = at(0), at(1), at(2)
            t2, a2 = at(3), at(4)
            t0, f0, a0 = t_p[edge, :], f_p[edge, :].astype(I32), a_p[edge, :]
            tl, tr = beside(t, patch_of(sides[0], p), lane)
            fl, fr = beside(f, patch_of(sides[1], p), lane)
            al, ar = beside(a, patch_of(sides[2], p), lane)
            tm, tp = at(0, -1), at(0, 1)
            f = f.astype(I32)
            low, high = (t2, t0) if side == 0 else (t0, t2)
            den = 1.0 + coef(f, 1, tl, tr, t) + coef(f, 2, low, high, t) + coef(f, 4, tm, tp, t)
            rden = 1.0 / den
            inward = (given_high if side == 0 else given_low)(f0, 2, t0, t)
            total = given_low(fl.astype(I32), 1, tl, t) * al
            total = total + given_high(fr.astype(I32), 1, tr, t) * ar
            total = total + given_low(at(1, -1).astype(I32), 4, tm, t) * at(2, -1)
            total = total + given_high(at(1, 1).astype(I32), 4, tp, t) * at(2, 1)
            total = total + jnp.maximum(t2 - t, 0.0) * a2 + inward * a0
            row_ref[0, side, p] = total * rden
            row_ref[1, side, p] = rden
            row_ref[2, side, p] = inward * rden


def sweeps_kernel(
    rec_ref, g_ref, rden_ref, x_ref, row_ref,
    last_ref, first_ref, second_ref, beyond_ref,
    turned, near, hot, main, wide, levels, adj, adj2, halo,
):
    for c in range(3):
        turned[c] = rec_ref[:, c * TX : (c + 1) * TX].T

    def records(g):
        base = GROUP * (g % 3)
        return [turned[g // 3, base + 8 * k : base + 8 * k + 8, :] for k in range(CAP)], turned[
            g // 3, base + 32 : base + 40, :
        ].astype(I32) - 1

    col8 = iota((TY, TX), 0)
    tall = iota((ROWS, TX), 0)
    across = iota((TX, TX), 0)
    deep = iota((Z, TX), 0)

    def ones(mask):
        return jnp.where(mask, 1.0, 0.0).astype(BF16)

    for dy in (-1, 0, 1):
        for n, dx in enumerate((-1, 0, 1)):
            g = NEAR.index((dx, dy))
            values, cells = records(g)
            for k in range(CAP):
                at = pl.ds((n * CAP + k) * TX, TX)
                cell = cells[k : k + 1, :]
                x = cell & (TX - 1)
                zy = cell >> 7
                if dy == 0:
                    hot[:, at] = ones(tall == zy)
                else:
                    z = jnp.where((zy & 7) == (7 if dy < 0 else 0), cell >> 10, -1)
                    levels[:, at] = ones(deep == z)
                column = (x + 4) & (TX - 1)
                wanted = (col8 == column) & (
                    (col8 < 4) if dx < 0 else (col8 >= 4) if dx > 0 else (col8 >= 0)
                )
                parts = split3(values[k])
                for m in range(3):
                    tiles = []
                    for side in range(2):
                        use = wanted
                        if dx == 0:
                            use = wanted & ((col8 >= 4) if side == 0 else (col8 < 4))
                        for s in range(SRC):
                            if dx == (1 if side == 0 else -1):
                                tiles.append(jnp.zeros((TY, TX), F32))
                            else:
                                tiles.append(jnp.where(use, parts[m][s : s + 1, :], 0.0))
                    near[m, :, at] = jnp.concatenate(tiles, axis=0).astype(BF16)
        onehot = hot[...] if dy == 0 else levels[...]
        strip = dot(onehot, near[0]) + dot(onehot, near[1]) + dot(onehot, near[2])
        if dy == 0:
            last_ref[SRC] = strip * rden_ref[SRC]
        else:
            side = 0 if dy < 0 else 1
            halo[side, SRC] = row_ref[0, side, SRC] + strip * row_ref[1, side, SRC]
            values, cells = records(NEAR.index((0, dy)))
            for k in range(CAP):
                at = pl.ds(k * TX, TX)
                cell = cells[k : k + 1, :]
                zy = cell >> 7
                z = jnp.where((zy & 7) == (7 if dy < 0 else 0), cell >> 10, -1)
                main[0, 0:TX, at] = ones(across == (cell & (TX - 1)))
                parts = split3(values[k])
                mask = deep == z
                for m in range(3):
                    wide[m, :, at] = jnp.concatenate(
                        [jnp.where(mask, parts[m][s : s + 1, :], 0.0) for s in range(SRC)], axis=0
                    ).astype(BF16)
            columns = main[0, 0:TX, :]
            got = dot(wide[0], columns) + dot(wide[1], columns) + dot(wide[2], columns)
            for s in range(SRC):
                halo[side, s] = (
                    row_ref[0, side, s] + got[s * Z : (s + 1) * Z, :] * row_ref[1, side, s]
                )

    values, cells = records(NEAR.index((0, 0)))
    for k in range(CAP):
        at = pl.ds(k * TX, TX)
        cell = cells[k : k + 1, :]
        mask = across == (cell & (TX - 1))
        parts = split3(values[k])
        for m in range(3):
            for s in range(SRC):
                main[m, s * TX : (s + 1) * TX, at] = jnp.where(
                    mask, parts[m][s : s + 1, :], 0.0
                ).astype(BF16)
    onehot = hot[:, CAP * TX : 2 * CAP * TX]
    for s in range(0, SRC, 2):
        two = slice(s * TX, (s + 2) * TX)
        got = dot(onehot, main[0, two, :]) + dot(onehot, main[1, two, :]) + dot(onehot, main[2, two, :])
        last_ref[s] = got[:, :TX] * rden_ref[s]
        last_ref[s + 1] = got[:, TX:] * rden_ref[s + 1]

    for p in range(PLANES):
        adj[p] = x_ref[p] + last_ref[p]
    lane = iota((TY, TX), 1)
    j = lane & 7
    row = iota((TY, TX), 0)

    def sweep(old, new, with_halo):
        def at_level(z, carry):
            here = level(z)
            below = level(jnp.maximum(z - 1, 0))
            above = level(jnp.minimum(z + 1, Z - 1))
            sides = both_sides(old[SRC, here, :], j)
            for p in range(PLANES):
                v = old[p, here, :]
                left, right = beside(v, patch_of(sides, p), lane)
                low, high = 0.0, 0.0
                if with_halo:
                    low = jnp.broadcast_to(halo[0, p, pl.ds(z, 1), :], (TY, TX))
                    high = jnp.broadcast_to(halo[1, p, pl.ds(z, 1), :], (TY, TX))
                down = jnp.where(row == 0, low, pltpu.roll(v, 1, 0))
                up = jnp.where(row == TY - 1, high, pltpu.roll(v, TY - 1, 0))
                total = last_ref[p, here, :]
                for k, w in enumerate((left, right, down, up, old[p, below, :], old[p, above, :])):
                    total = total + g_ref[k, p, here, :] * w
                new[p, here, :] = total
            return carry

        lax.fori_loop(0, Z, at_level, 0)

    sweep(adj, adj2, True)
    sweep(adj2, last_ref, False)

    low, high = pl.ds(0, Z, stride=TY), pl.ds(TY - 1, Z, stride=TY)

    def pack(out, edge):
        total = None
        for p in range(PLANES):
            out[p] = adj2[p, edge, :]
            if p < SRC:
                part = last_ref[p, edge, :]
                total = part if total is None else total + part
        out[PLANES] = total

    even_y = is_even("gy")

    @pl.when(even_y)
    def _():
        pack(first_ref, high)
        pack(second_ref, low)

    @pl.when(jnp.logical_not(even_y))
    def _():
        pack(first_ref, low)
        pack(second_ref, high)

    for side, edge in enumerate((low, high)):
        total = None
        for s in range(SRC):
            part = row_ref[2, side, s] * adj2[s, edge, :]
            total = part if total is None else total + part
        beyond_ref[side] = total


def gradient_kernel(
    last_ref, y0_ref, y1_ref, edge_ref, beyond_ref, slow_ref, adj_ref, grad_ref, fix, above
):
    even_y = is_even("gy")
    for p in range(PLANES + 1):
        first, second = y0_ref[p], y1_ref[p]
        from_low = jnp.where(even_y, second, first)
        from_high = jnp.where(even_y, first, second)
        if p < PLANES:
            fix[0, p] = edge_ref[0, p] * from_low
            fix[1, p] = edge_ref[1, p] * from_high
        else:
            above[0] = beyond_ref[0] + from_low
            above[1] = beyond_ref[1] + from_high
    lane = iota((TY, TX), 1)
    row = iota((TY, TX), 0)

    def at_level(z, carry):
        here = level(z)

        def wide(ref, *index):
            return jnp.broadcast_to(ref[(*index, pl.ds(z, 1), slice(None))], (TY, TX))

        total = None
        for p in range(PLANES):
            v = last_ref[p, here, :]
            v = v + jnp.where(row == 0, wide(fix, 0, p), jnp.where(row == TY - 1, wide(fix, 1, p), 0.0))
            if p < SRC:
                adj_ref[p, here, :] = v
                total = v if total is None else total + v
            else:
                strip = v
        for by in (8, 16, 32):
            strip = strip + turn(strip, by)
        left = jnp.where(lane == 0, turn(strip, -59), turn(total, 1))
        right = jnp.where(lane == TX - 1, turn(strip, 3), turn(total, -1))
        down = jnp.where(row == 0, wide(above, 0), pltpu.roll(total, 1, 0))
        up = jnp.where(row == TY - 1, wide(above, 1), pltpu.roll(total, TY - 1, 0))
        beside_it = right + left + up + down
        grad_ref[here, :] = slow_ref[here, :] * (total + 0.125 * (beside_it - 4.0 * total))
        return carry

    lax.fori_loop(0, Z, at_level, 0)


def call(kernel, outs, scratch, flops, name):
    vmem = pl.BlockSpec(memory_space=pltpu.VMEM)

    def run(*args):
        moved = sum(a.size * 4 for a in args)
        return pl.pallas_call(
            kernel,
            name=name,
            out_shape=[jax.ShapeDtypeStruct(s, F32) for s in outs],
            in_specs=[vmem] * len(args),
            out_specs=[vmem] * len(outs),
            scratch_shapes=scratch,
            compiler_params=pltpu.CompilerParams(vmem_limit_bytes=24 << 20),
            cost_estimate=pl.CostEstimate(flops=flops, bytes_accessed=moved, transcendentals=0),
        )(*args)

    return run


def swapped(v, axis, count, odd):
    pairs = [(i, i + 1) for i in range(odd, count - 1, 2)]
    return lax.ppermute(v, axis, [(a, b) for a, b in pairs] + [(b, a) for a, b in pairs])


def shards(traveltime, adjoint_start, upwind_flags, slowness, residual_rows, station_tile, station_cell):
    devices = lax.axis_size(("gx", "gy"))
    nx, ny = lax.axis_size("gx"), lax.axis_size("gy")
    count = residual_rows.shape[0]
    t, a, f = (v.reshape(SRC, ROWS, TX) for v in (traveltime, adjoint_start, upwind_flags))

    (sent,) = call(
        records_kernel,
        [(devices, 3 * TX)],
        [pltpu.VMEM((3, GROUP, count), F32), pltpu.VMEM((devices + 64, TX), F32)],
        10**6,
        "records",
    )(residual_rows.T, station_tile.reshape(1, count), station_cell.reshape(1, count))

    x_out0, x_out1, own = call(
        edges_kernel, [(ROWS, TX), (ROWS, TX), (3, ROWS, TX)], [], 10**6, "edges"
    )(t, a, f)
    x_in0 = swapped(x_out0, "gx", nx, 0)
    x_in1 = swapped(x_out1, "gx", nx, 1)

    strip, y_out0, y_out1 = call(
        strips_kernel,
        [(3, ROWS, TX), (5, PLANES, Z, TX), (5, PLANES, Z, TX)],
        [],
        10**6,
        "strips",
    )(t, a, f, own, x_in0, x_in1)
    y_in0 = swapped(y_out0, "gy", ny, 0)
    y_in1 = swapped(y_out1, "gy", ny, 1)

    got = lax.all_to_all(sent, ("gx", "gy"), 0, 0, tiled=True)

    g, rden, x1, edge, halo_rows = call(
        coefficients_kernel,
        [
            (6, PLANES, ROWS, TX),
            (PLANES, ROWS, TX),
            (PLANES, ROWS, TX),
            (2, PLANES, Z, TX),
            (3, 2, PLANES, Z, TX),
        ],
        [pltpu.VMEM((2, 5, PLANES, Z + 2 * PAD, TX), F32)],
        10**7,
        "coefficients",
    )(t, a, f, strip, y_in0, y_in1)

    depth = CAP * TX
    last, e_out0, e_out1, beyond = call(
        sweeps_kernel,
        [
            (PLANES, ROWS, TX),
            (PLANES + 1, Z, TX),
            (PLANES + 1, Z, TX),
            (2, Z, TX),
        ],
        [
            pltpu.VMEM((3, TX, TX), F32),
            pltpu.VMEM((3, TX, 3 * depth), BF16),
            pltpu.VMEM((ROWS, 3 * depth), BF16),
            pltpu.VMEM((3, SRC * TX, depth), BF16),
            pltpu.VMEM((3, SRC * Z, depth), BF16),
            pltpu.VMEM((Z, 3 * depth), BF16),
            pltpu.VMEM((PLANES, ROWS, TX), F32),
            pltpu.VMEM((PLANES, ROWS, TX), F32),
            pltpu.VMEM((2, PLANES, Z, TX), F32),
        ],
        10**7,
        "sweeps",
    )(got, g, rden, x1, halo_rows)
    e_in0 = swapped(e_out0, "gy", ny, 0)
    e_in1 = swapped(e_out1, "gy", ny, 1)

    adjoint, gradient = call(
        gradient_kernel,
        [(SRC, ROWS, TX), (ROWS, TX)],
        [pltpu.VMEM((2, PLANES, Z, TX), F32), pltpu.VMEM((2, Z, TX), F32)],
        10**6,
        "gradient",
    )(last, e_in0, e_in1, edge, beyond, slowness.reshape(ROWS, TX))
    return adjoint.reshape(traveltime.shape), gradient.reshape(slowness.shape)


def solution(mesh):
    placed = (
        P(None, None, "gy", "gx"),
        P(None, None, "gy", "gx"),
        P(None, None, "gy", "gx"),
        P(None, "gy", "gx"),
        P(("gx", "gy"), None),
        P(("gx", "gy"), None),
        P(("gx", "gy")),
    )
    return jax.shard_map(
        shards,
        mesh=mesh,
        in_specs=placed,
        out_specs=(P(None, None, "gy", "gx"), P(None, "gy", "gx")),
        check_vma=False,
    )
```

profile of v0, /device:TPU:23, one launch (start us, length us, event | category | flops | bytes accessed | tf_op | source)
XLA Modules:
  0.0 87.7 jit_solution(159869176986196885)
XLA Ops:
  0.6 0.0 copy-start
  0.6 1.2 %copy-done = f32[8,32,8,128]{3,2,1,0:T(8,128)S(1)} copy-done((f32[8,32,8,128]{3,2,1,0:T(8,128)S(1)}, f32[8,32,8,128]{3,2,1,0:T(8,128)}, u32[]{:S(2)}) %copy-start) | copy-done | bytes 1048600
  1.9 0.0 copy-start.2
  1.9 1.2 %copy-done.2 = f32[8,32,8,128]{3,2,1,0:T(8,128)S(1)} copy-done((f32[8,32,8,128]{3,2,1,0:T(8,128)S(1)}, f32[8,32,8,128]{3,2,1,0:T(8,128)}, u32[]{:S(2)}) %copy-start.2) | copy-done | bytes 1048600
  3.1 0.0 copy-start.3
  3.1 1.2 %copy-done.3 = s32[8,32,8,128]{3,2,1,0:T(8,128)S(1)} copy-done((s32[8,32,8,128]{3,2,1,0:T(8,128)S(1)}, s32[8,32,8,128]{3,2,1,0:T(8,128)}, u32[]{:S(2)}) %copy-start.3) | copy-done | bytes 1048600
  4.3 3.0 %edges.1 = (f32[256,128]{1,0:T(8,128)S(1)}, f32[256,128]{1,0:T(8,128)S(1)}, f32[3,256,128]{2,1,0:T(8,128)S(1)}) custom-call(f32[8,256,128]{2,1,0:T(8,128)S(1)} %bitcast.13, f32[8,256,128]{2,1,0:T(8,128)S(1)} %bitcast.16, s32[8,256,128]{2,1,0:T(8,128)S(1)} %bitcast.19), custom_call_target="tpu_custom_call" | custom-call | flops 1000000 | bytes 3145728 | tf_op jit(solution)/shard_map/edges/pallas_call | solution.py:522
  7.3 3.6 %collective-permute-start = (f32[256,128]{1,0:T(8,128)S(1)}, f32[256,128]{1,0:T(8,128)S(1)}, u32[]{:S(2)}, u32[]{:S(2)}) collective-permute-start(f32[256,128]{1,0:T(8,128)S(1)} %get-tuple-element.20), channel_id=1, source_target_pairs={{0,16},{32,48},{64,80},{96,112},{16,0},{48,32},{80,64},{112,96},{1... | collective-permute-start | bytes 393224 | tf_op jit(solution)/shard_map/ppermute | solution.py:538
  10.9 2.2 %collective-permute-start.1 = (f32[256,128]{1,0:T(8,128)S(1)}, f32[256,128]{1,0:T(8,128)S(1)}, u32[]{:S(2)}, u32[]{:S(2)}) collective-permute-start(f32[256,128]{1,0:T(8,128)S(1)} %get-tuple-element.21), channel_id=1, source_target_pairs={{16,32},{48,64},{80,96},{32,16},{64,48},{96,80},{17,33},{49,65},{8... | collective-permute-start | bytes 393224 | tf_op jit(solution)/shard_map/ppermute | solution.py:538
  13.1 1.0 %collective-permute-done.x0_ref = f32[256,128]{1,0:T(8,128)S(1)} collective-permute-done((f32[256,128]{1,0:T(8,128)S(1)}, f32[256,128]{1,0:T(8,128)S(1)}, u32[]{:S(2)}, u32[]{:S(2)}) %collective-permute-start) | collective-permute-done | bytes 131104 | tf_op jit(solution)/shard_map/ppermute | solution.py:538
  14.1 4.9 %collective-permute-done.1.x1_ref = f32[256,128]{1,0:T(8,128)S(1)} collective-permute-done((f32[256,128]{1,0:T(8,128)S(1)}, f32[256,128]{1,0:T(8,128)S(1)}, u32[]{:S(2)}, u32[]{:S(2)}) %collective-permute-start.1) | collective-permute-done | bytes 131104 | tf_op jit(solution)/shard_map/ppermute | solution.py:538
  19.0 0.0 copy-start.5
  19.0 0.0 copy-start.6
  19.0 0.0 copy-start.7
  19.0 2.6 %strips.1 = (f32[3,256,128]{2,1,0:T(8,128)S(1)}, f32[5,9,32,128]{3,2,1,0:T(8,128)S(1)}, f32[5,9,32,128]{3,2,1,0:T(8,128)S(1)}) custom-call(f32[8,256,128]{2,1,0:T(8,128)S(1)} %bitcast.14, f32[8,256,128]{2,1,0:T(8,128)S(1)} %bitcast.17, s32[8,256,128]{2,1,0:T(8,128)S(1)} %bitcast.20, f32[3,256,128]{2,1,0:T(8,128)S(1)} %get-tuple-element.19.own_ref, ...), custom_call_target="tpu_custom_call" | custom-call | flops 1000000 | bytes 3801088 | tf_op jit(solution)/shard_map/strips/pallas_call | solution.py:522
  21.6 0.0 copy-start.1
  21.6 2.2 %collective-permute-start.2 = (f32[5,9,32,128]{3,2,1,0:T(8,128)S(1)}, f32[5,9,32,128]{3,2,1,0:T(8,128)S(1)}, u32[]{:S(2)}, u32[]{:S(2)}) collective-permute-start(f32[5,9,32,128]{3,2,1,0:T(8,128)S(1)} %get-tuple-element.23), channel_id=1, source_target_pairs={{0,1},{2,3},{4,5},{6,7},{8,9},{10,11},{12,13},{14,15},{1,0},{3,2},... | collective-permute-start | bytes 2211848 | tf_op jit(solution)/shard_map/ppermute | solution.py:538
  23.8 2.7 %collective-permute-start.3 = (f32[5,9,32,128]{3,2,1,0:T(8,128)S(1)}, f32[5,9,32,128]{3,2,1,0:T(8,128)S(1)}, u32[]{:S(2)}, u32[]{:S(2)}) collective-permute-start(f32[5,9,32,128]{3,2,1,0:T(8,128)S(1)} %get-tuple-element.24), channel_id=1, source_target_pairs={{1,2},{3,4},{5,6},{7,8},{9,10},{11,12},{13,14},{2,1},{4,3},{6,5},{... | collective-permute-start | bytes 2211848 | tf_op jit(solution)/shard_map/ppermute | solution.py:538
  26.5 0.0 copy-done.5
  26.5 0.0 copy-done.6
  26.5 0.0 copy-done.7
  26.6 0.6 records.1
  27.1 0.2 copy.9
  27.3 19.5 %all_to_all.11 = f32[128,1,384]{2,1,0:T(1,128)S(1)} all-to-all(f32[128,1,384]{2,1,0:T(1,128)S(1)} %copy.9), channel_id=1, replica_groups=mesh['gx'=8,'gy'=16] {'gx','gy'}, dimensions={0} | all-to-all | bytes 393216 | tf_op jit(solution)/shard_map/all_to_all | solution.py:571
  46.9 0.0 collective-permute-done.2.y0_ref
  46.9 0.0 collective-permute-done.3.y1_ref
  46.9 0.0 copy-done.1
  46.9 8.0 %coefficients.1 = (f32[6,9,256,128]{3,2,1,0:T(8,128)S(1)}, f32[9,256,128]{2,1,0:T(8,128)S(1)}, f32[9,256,128]{2,1,0:T(8,128)S(1)}, f32[2,9,32,128]{3,2,1,0:T(8,128)S(1)}, f32[3,2,9,32,128]{4,3,2,1,0:T(8,128)S(1)}) custom-call(f32[8,256,128]{2,1,0:T(8,128)S(1)} %bitcast.15, f32[8,256,128]{2,1,0:T(8,128)S(1)} %bitcast.18, s32[8,256,128]{2,1,0:T(8,128)S(1)} %bitcast.21, ...), custom_call_target="tpu_custom_call" | custom-call | flops 10000000 | bytes 5013504 | tf_op jit(solution)/shard_map/coefficients/pallas_call | solution.py:522
  54.9 0.0 copy-start.4
  54.9 14.0 %sweeps.1 = (f32[9,256,128]{2,1,0:T(8,128)S(1)}, f32[10,32,128]{2,1,0:T(8,128)S(1)}, f32[10,32,128]{2,1,0:T(8,128)S(1)}, f32[2,32,128]{2,1,0:T(8,128)S(1)}) custom-call(f32[128,384]{1,0:T(8,128)S(1)} %bitcast.23, f32[6,9,256,128]{3,2,1,0:T(8,128)S(1)} %get-tuple-element.25.g_ref, f32[9,256,128]{2,1,0:T(8,128)S(1)} %get-tuple-element.26.rden_ref, ...), custom_call_target="tpu_custom_call" | custom-call | flops 10000000 | bytes 10518528 | tf_op jit(solution)/shard_map/sweeps/pallas_call | solution.py:522
  68.9 0.5 collective-permute-start.4
  69.4 2.1 %collective-permute-start.5 = (f32[10,32,128]{2,1,0:T(8,128)S(1)}, f32[10,32,128]{2,1,0:T(8,128)S(1)}, u32[]{:S(2)}, u32[]{:S(2)}) collective-permute-start(f32[10,32,128]{2,1,0:T(8,128)S(1)} %get-tuple-element.31), channel_id=1, source_target_pairs={{1,2},{3,4},{5,6},{7,8},{9,10},{11,12},{13,14},{2,1},{4,3},{6,5},{... | collective-permute-start | bytes 491528 | tf_op jit(solution)/shard_map/ppermute | solution.py:538
  71.5 0.0 collective-permute-done.4.y0_ref
  71.5 6.3 %collective-permute-done.5.y1_ref = f32[10,32,128]{2,1,0:T(8,128)S(1)} collective-permute-done((f32[10,32,128]{2,1,0:T(8,128)S(1)}, f32[10,32,128]{2,1,0:T(8,128)S(1)}, u32[]{:S(2)}, u32[]{:S(2)}) %collective-permute-start.5) | collective-permute-done | bytes 163872 | tf_op jit(solution)/shard_map/ppermute | solution.py:538
  77.7 0.0 copy-done.4
  77.7 10.0 %gradient.1 = (f32[8,256,128]{2,1,0:T(8,128)}, f32[256,128]{1,0:T(8,128)}) custom-call(f32[9,256,128]{2,1,0:T(8,128)S(1)} %get-tuple-element.29.last_ref, f32[10,32,128]{2,1,0:T(8,128)S(1)} %collective-permute-done.4.y0_ref, f32[10,32,128]{2,1,0:T(8,128)S(1)} %collective-permute-done.5.y1_ref, f32[2,9,32,128]{3,2,1,0:T(8,128)S(1)} %get-tuple-element.32.edge_ref, ...), custom_call_target="tpu_custom_call" | custom-call | flops 1000000 | bytes 1966080 | tf_op jit(solution)/shard_map/gradient/pallas_call | solution.py:522
  (1 shorter events, 0.0 us)
Async XLA Ops:
  0.6 1.2 %copy-start = (f32[8,32,8,128]{3,2,1,0:T(8,128)S(1)}, f32[8,32,8,128]{3,2,1,0:T(8,128)}, u32[]{:S(2)}) copy-start(f32[8,32,8,128]{3,2,1,0:T(8,128)} %param.7) | copy-start | bytes 3145732
  1.9 1.2 %copy-start.2 = (f32[8,32,8,128]{3,2,1,0:T(8,128)S(1)}, f32[8,32,8,128]{3,2,1,0:T(8,128)}, u32[]{:S(2)}) copy-start(f32[8,32,8,128]{3,2,1,0:T(8,128)} %param.8) | copy-start | bytes 3145732
  3.1 1.2 %copy-start.3 = (s32[8,32,8,128]{3,2,1,0:T(8,128)S(1)}, s32[8,32,8,128]{3,2,1,0:T(8,128)}, u32[]{:S(2)}) copy-start(s32[8,32,8,128]{3,2,1,0:T(8,128)} %param.9) | copy-start | bytes 3145732
  7.3 6.8 %collective-permute-start = (f32[256,128]{1,0:T(8,128)S(1)}, f32[256,128]{1,0:T(8,128)S(1)}, u32[]{:S(2)}, u32[]{:S(2)}) collective-permute-start(f32[256,128]{1,0:T(8,128)S(1)} %get-tuple-element.20), channel_id=1, source_target_pairs={{0,16},{32,48},{64,80},{96,112},{16,0},{48,32},{80,64},{112,96},{1... | collective-permute-start | bytes 393224 | tf_op jit(solution)/shard_map/ppermute | solution.py:538
  10.9 8.1 %collective-permute-start.1 = (f32[256,128]{1,0:T(8,128)S(1)}, f32[256,128]{1,0:T(8,128)S(1)}, u32[]{:S(2)}, u32[]{:S(2)}) collective-permute-start(f32[256,128]{1,0:T(8,128)S(1)} %get-tuple-element.21), channel_id=1, source_target_pairs={{16,32},{48,64},{80,96},{32,16},{64,48},{96,80},{17,33},{49,65},{8... | collective-permute-start | bytes 393224 | tf_op jit(solution)/shard_map/ppermute | solution.py:538
  19.0 7.5 %copy-start.5 = (f32[256,8]{0,1:T(8,128)S(1)}, f32[256,8]{0,1:T(8,128)}, u32[]{:S(2)}) copy-start(f32[256,8]{0,1:T(8,128)} %param.11) | copy-start | bytes 24580
  19.0 7.5 %copy-start.6 = (s32[256,1]{0,1:T(1,128)S(1)}, s32[256,1]{0,1:T(1,128)}, u32[]{:S(2)}) copy-start(s32[256,1]{0,1:T(1,128)} %param.12) | copy-start | bytes 3076
  19.0 7.5 %copy-start.7 = (s32[256]{0:T(256)S(1)}, s32[256]{0:T(256)}, u32[]{:S(2)}) copy-start(s32[256]{0:T(256)} %param.13) | copy-start | bytes 3076
  21.6 25.3 %copy-start.1 = (f32[8,32,8,128]{3,2,1,0:T(8,128)S(1)}, f32[8,32,8,128]{3,2,1,0:T(8,128)}, u32[]{:S(2)}) copy-start(f32[8,32,8,128]{3,2,1,0:T(8,128)} %param.7) | copy-start | bytes 3145732
  21.6 25.2 %collective-permute-start.2 = (f32[5,9,32,128]{3,2,1,0:T(8,128)S(1)}, f32[5,9,32,128]{3,2,1,0:T(8,128)S(1)}, u32[]{:S(2)}, u32[]{:S(2)}) collective-permute-start(f32[5,9,32,128]{3,2,1,0:T(8,128)S(1)} %get-tuple-element.23), channel_id=1, source_target_pairs={{0,1},{2,3},{4,5},{6,7},{8,9},{10,11},{12,13},{14,15},{1,0},{3,2},... | collective-permute-start | bytes 2211848 | tf_op jit(solution)/shard_map/ppermute | solution.py:538
  23.8 23.1 %collective-permute-start.3 = (f32[5,9,32,128]{3,2,1,0:T(8,128)S(1)}, f32[5,9,32,128]{3,2,1,0:T(8,128)S(1)}, u32[]{:S(2)}, u32[]{:S(2)}) collective-permute-start(f32[5,9,32,128]{3,2,1,0:T(8,128)S(1)} %get-tuple-element.24), channel_id=1, source_target_pairs={{1,2},{3,4},{5,6},{7,8},{9,10},{11,12},{13,14},{2,1},{4,3},{6,5},{... | collective-permute-start | bytes 2211848 | tf_op jit(solution)/shard_map/ppermute | solution.py:538
  54.9 22.8 %copy-start.4 = (f32[32,8,128]{2,1,0:T(8,128)S(1)}, f32[32,8,128]{2,1,0:T(8,128)}, u32[]{:S(2)}) copy-start(f32[32,8,128]{2,1,0:T(8,128)} %param.10) | copy-start | bytes 393220
  68.9 2.6 %collective-permute-start.4 = (f32[10,32,128]{2,1,0:T(8,128)S(1)}, f32[10,32,128]{2,1,0:T(8,128)S(1)}, u32[]{:S(2)}, u32[]{:S(2)}) collective-permute-start(f32[10,32,128]{2,1,0:T(8,128)S(1)} %get-tuple-element.30), channel_id=1, source_target_pairs={{0,1},{2,3},{4,5},{6,7},{8,9},{10,11},{12,13},{14,15},{1,0},{3,2},... | collective-permute-start | bytes 491528 | tf_op jit(solution)/shard_map/ppermute | solution.py:538
  69.4 8.4 %collective-permute-start.5 = (f32[10,32,128]{2,1,0:T(8,128)S(1)}, f32[10,32,128]{2,1,0:T(8,128)S(1)}, u32[]{:S(2)}, u32[]{:S(2)}) collective-permute-start(f32[10,32,128]{2,1,0:T(8,128)S(1)} %get-tuple-element.31), channel_id=1, source_target_pairs={{1,2},{3,4},{5,6},{7,8},{9,10},{11,12},{13,14},{2,1},{4,3},{6,5},{... | collective-permute-start | bytes 491528 | tf_op jit(solution)/shard_map/ppermute | solution.py:538
where the time goes:
time: 88 us; the launch traced here: 87.7 us
  Pallas kernels  38 us (43%)
  blocking collectives  19.5 us (22%)
  starting transfers between devices  13.2 us (15%)
  waiting for transfers between devices  12.2 us (14%)
  local copies, waits for them, and re-layouts  3.91 us (4%)
    pallas_call x6, Pallas kernels, run(): pl.pallas_call(kernel, name=name, out_shape=[jax.ShapeDtypeStruct(s, F32)...  38 us
    all_to_all x1, blocking collectives, shards(): got = lax.all_to_all(sent, ('gx', 'gy'), 0, 0, tiled=True)  19.5 us
    ppermute x6, starting transfers between devices, swapped(): lax.ppermute(v, axis, [(a, b) for a, b in pairs] + [(b, a) for a, b in pa...  13.2 us
    ppermute x6, waiting for transfers between devices, swapped(): lax.ppermute(v, axis, [(a, b) for a, b in pairs] + [(b, a) for a, b in pa...  12.2 us
    unnamed x17, local copies, waits for them, and re-layouts  3.71 us
  transfers between devices with their start and end apart: 6, of which 3 were waited for; matrix products, arithmetic and copies ran while one was open for 0% of the time, Pallas kernels for 1%

commit v1 on v0

v1 whole, which is shorter than its diff:
```python
import jax
import jax.numpy as jnp
from jax import lax
from jax.experimental import pallas as pl
from jax.experimental.pallas import tpu as pltpu
from jax.sharding import PartitionSpec as P


F32 = jnp.float32
BF16 = jnp.bfloat16
I32 = jnp.int32

SRC = 8
Z = 32
TY = 8
TX = 128
PLANES = SRC + 1
ROWS = Z * TY
HALO = 4
CAP = 4
SPLIT = 2
GROUP = 40
PART = 64
LEAVING_LIMIT = 52
RECORDS_LIMIT = 56
CORE_LIMIT = 51
PAD = 8
NEAR = tuple((dx, dy) for dx in (-1, 0, 1) for dy in (-1, 0, 1))

NT = (((1,), (1,)), ((), ()))
NN = (((1,), (0,)), ((), ()))


def iota(shape, dim):
    return lax.broadcasted_iota(I32, shape, dim)


def turn(v, by):
    return pltpu.roll(v, by % TX, 1)


def level(z):
    return pl.ds(pl.multiple_of(z * TY, TY), TY)


def cat(parts):
    return jnp.concatenate(parts, axis=0)


def dot(a, b, dims=NT):
    return lax.dot_general(a, b, dims, preferred_element_type=F32)


def split(v, count):
    parts = []
    for _ in range(count - 1):
        parts.append(v.astype(BF16).astype(F32))
        v = v - parts[-1]
    return [*parts, v]


def all_start(copies):
    for copy in copies:
        copy.start()


def all_wait(copies):
    for copy in copies:
        copy.wait()


def is_even(axis):
    return lax.rem(lax.axis_index(axis), 2) == 0


def records_kernel(
    rows_hbm, tile_hbm, cell_hbm, out_ref, rows_ref, tile_ref, cell_ref, parts, shifted, sems
):
    pairs = ((tile_hbm, tile_ref), (rows_hbm, rows_ref), (cell_hbm, cell_ref))
    coming = [pltpu.make_async_copy(hbm, ref, sems.at[n]) for n, (hbm, ref) in enumerate(pairs)]
    all_start(coming)
    shifted[...] = jnp.zeros(shifted.shape, F32)
    count = rows_ref.shape[1]
    devices = out_ref.shape[0] // 3
    all_wait(coming)
    named = (iota((devices, count), 0) == tile_ref[...]).astype(F32)
    earlier = (iota((count, count), 0) < iota((count, count), 1)).astype(F32).astype(BF16)
    picks = named.astype(BF16)
    before = dot(picks, earlier, NN)
    rank = jnp.sum(before * named, axis=0, keepdims=True).astype(I32)
    values = rows_ref[...]
    cells = (cell_ref[...] + 1).astype(F32)
    blocks = [jnp.where(rank == k, values, 0.0) for k in range(CAP)]
    blocks.append(jnp.where(rank == iota((8, count), 0), cells, 0.0))
    for k, block in enumerate(blocks):
        for n, part in enumerate(split(block, 3)):
            parts[n, 8 * k : 8 * k + 8, :] = part
    own = sum(dot(picks, parts[n].astype(BF16)) for n in range(3))
    shifted[32 : 32 + devices, 0:GROUP] = own
    lane = iota((devices, TX), 1)
    ty = lax.rem(iota((devices, TX), 0), 16)
    for c in range(3):
        chunk = jnp.zeros((devices, TX), F32)
        for i in range(3):
            dx, dy = NEAR[3 * c + i]
            off = 32 + 16 * dx + dy
            theirs = shifted[off : off + devices, :]
            held = (lane >= GROUP * i) & (lane < GROUP * (i + 1))
            if dy:
                held = held & (ty + dy >= 0) & (ty + dy < 16)
            chunk = jnp.where(held, turn(theirs, GROUP * i) if i else theirs, chunk)
        out_ref[pl.ds(c, devices, stride=3), :] = chunk


def edge_rows(out, t, a, f, high):
    edge = pl.ds(TY - 1 if high else 0, Z, stride=TY)
    inner = pl.ds(TY - 2 if high else 1, Z, stride=TY)
    out[0][...] = t[edge, :]
    out[1][...] = f[edge, :].astype(F32)
    out[2][...] = a[edge, :]
    out[3][...] = t[inner, :]
    up = (f[inner, :] & 2) != 0
    given = a[inner, :]
    out[4][...] = jnp.where(up, given, 0.0) if high else jnp.where(up, 0.0, given)


def by_parity(axis, first, second, fill):
    even = is_even(axis)

    @pl.when(even)
    def _():
        fill(first, True)
        fill(second, False)

    @pl.when(jnp.logical_not(even))
    def _():
        fill(first, False)
        fill(second, True)


def leaving_kernel(
    t_hbm, a_hbm, f_hbm,
    x0_ref, x1_ref, y0_ref, y1_ref, own_ref,
    t_ref, a_ref, f_ref, sems,
):
    arrays = ((t_hbm, t_ref), (a_hbm, a_ref), (f_hbm, f_ref))

    def copies(c):
        part = pl.ds(c * PART, PART)
        return [
            pltpu.make_async_copy(hbm.at[:, part, :], ref.at[:, part, :], sems.at[n, c])
            for n, (hbm, ref) in enumerate(arrays)
        ]

    for c in range(ROWS // PART):
        for copy in copies(c):
            copy.start()

    even = is_even("gx")
    lane = iota((TY, TX), 1)
    j = lane & 7

    def at_level(z, carry):
        here = level(z)
        packed = []
        for n, ref in enumerate((t_ref, a_ref, f_ref)):
            both = None
            for s in range(SRC):
                v = turn(ref[s, here, :].astype(F32), HALO + 8 * s)
                both = v if both is None else jnp.where(lane >> 3 == s, v, both)
            own_ref[n, here, :] = both
            packed.append(both)
        t, a, f = packed
        f = turn(f, 64)
        to_right = jnp.where(lane < 64, jnp.where(j < 4, t, turn(a, 4)), f)
        to_left = jnp.where(lane < 64, jnp.where(j < 4, turn(t, -4), a), f)
        x0_ref[here, :] = jnp.where(even, to_right, to_left)
        x1_ref[here, :] = jnp.where(even, to_left, to_right)
        return carry

    for c in range(ROWS // PART):
        for copy in copies(c):
            copy.wait()
        levels = PART // TY
        lax.fori_loop(c * levels, (c + 1) * levels, at_level, 0, unroll=8)

    def rows(out, high):
        for p in range(SRC):
            edge_rows([out.at[k, p] for k in range(5)], t_ref.at[p], a_ref.at[p], f_ref.at[p], high)

    by_parity("gy", y0_ref, y1_ref, rows)


def strips_kernel(
    own_ref, x0_ref, x1_ref, strip_out, y0_ref, y1_ref, strip_ref, f_ref, sems
):
    even = is_even("gx")
    shape = (ROWS, TX)
    lane = iota(shape, 1)
    near = (lane & 7) < 4
    low = lane < 64
    x0, x1 = x0_ref[...], x1_ref[...]
    left = jnp.where(even, x1, x0)
    right = jnp.where(even, x0, x1)
    t, a, f = own_ref[0], own_ref[1], own_ref[2]
    strip_ref[0] = jnp.where(
        low, jnp.where(near, left, t), turn(jnp.where(near, t, turn(right, 4)), 64)
    )
    strip_ref[1] = jnp.where(
        low, jnp.where(near, turn(left, -4), a), turn(jnp.where(near, a, right), 64)
    )
    flags = jnp.where(low, jnp.where(near, turn(left, 64), f), jnp.where(near, turn(f, 64), right))
    strip_ref[2] = flags
    f_ref[...] = flags.astype(I32)
    going = pltpu.make_async_copy(strip_ref, strip_out, sems.at[0])
    going.start()

    def rows(out, high):
        edge_rows([out.at[k] for k in range(5)], strip_ref.at[0], strip_ref.at[1], f_ref, high)

    by_parity("gy", y0_ref, y1_ref, rows)
    going.wait()


def both_sides(strip):
    return jnp.where((iota(strip.shape, 1) & 7) == 3, strip, turn(strip, 62))


def beside(v, patch, lane):
    if patch is None:
        return turn(v, 1), turn(v, -1)
    return jnp.where(lane == 0, patch, turn(v, 1)), jnp.where(lane == TX - 1, patch, turn(v, -1))


def patch_of(sides, p):
    return None if p == SRC else turn(sides, -(8 * p + 3))


def given_low(flag, bit, theirs, mine):
    return jnp.where((flag & bit) != 0, jnp.maximum(theirs - mine, 0.0), 0.0)


def given_high(flag, bit, theirs, mine):
    return jnp.where((flag & bit) == 0, jnp.maximum(theirs - mine, 0.0), 0.0)


def coef(flag, bit, low, high, mine):
    return jnp.maximum(mine - jnp.where((flag & bit) != 0, high, low), 0.0)


def take_rows(first, second, rows, flags, p, k):
    even = is_even("gy")
    here = pl.ds(PAD, Z)
    for side in range(2):
        v = jnp.where(even, second, first) if side == 0 else jnp.where(even, first, second)
        if k == 1:
            flags[side, p, here, :] = v.astype(I32)
        else:
            rows[side, k, p, here, :] = v


def shares_at(z, p, refs, sides, rows, flags, lane, row):
    t_p, a_p, f_p = refs
    here = level(z)
    below = level(jnp.maximum(z - 1, 0))
    above = level(jnp.minimum(z + 1, Z - 1))

    def halo(ref, *index):
        return jnp.broadcast_to(ref[(*index, pl.ds(PAD + z, 1), slice(None))], (TY, TX))

    def down(v, h):
        return jnp.where(row == 0, h, pltpu.roll(v, 1, 0))

    def up(v, h):
        return jnp.where(row == TY - 1, h, pltpu.roll(v, TY - 1, 0))

    t, f, a = t_p[here, :], f_p[here, :], a_p[here, :]
    tl, tr = beside(t, sides[0], lane)
    al, ar = beside(a, sides[1], lane)
    fl, fr = beside(f, sides[2], lane)
    tu, td = down(t, halo(rows, 0, 0, p)), up(t, halo(rows, 1, 0, p))
    fu, fd = down(f, halo(flags, 0, p)), up(f, halo(flags, 1, p))
    au, ad = down(a, halo(rows, 0, 2, p)), up(a, halo(rows, 1, 2, p))
    tm = jnp.where(z > 0, t_p[below, :], 0.0)
    tp = jnp.where(z < Z - 1, t_p[above, :], 0.0)
    den = 1.0 + coef(f, 1, tl, tr, t) + coef(f, 2, tu, td, t) + coef(f, 4, tm, tp, t)
    rden = 1.0 / den
    shares = [
        given_low(fl, 1, tl, t),
        given_high(fr, 1, tr, t),
        given_low(fu, 2, tu, t),
        given_high(fd, 2, td, t),
        given_low(f_p[below, :], 4, tm, t),
        given_high(f_p[above, :], 4, tp, t),
    ]
    shares = [g * rden for g in shares]
    total = None
    for g, v in zip(shares, (al, ar, au, ad, a_p[below, :], a_p[above, :])):
        total = g * v if total is None else total + g * v
    return shares, rden, total


def ones(mask):
    return jnp.where(mask, 1.0, 0.0).astype(BF16)


def scatter(rec_ref, main_ref, strip_ref, row_ref, turned, hot, levels, near, wide, spots):
    for c in range(3):
        turned[c] = rec_ref[pl.ds(c, TX, stride=3), :].T

    def held(dx, dy):
        g = NEAR.index((dx, dy))
        base = GROUP * (g % 3)
        values = [turned[g // 3, base + 8 * k : base + 8 * k + 8, :] for k in range(CAP)]
        return values, turned[g // 3, base + 32 : base + 40, :].astype(I32) - 1

    j = iota((TY, TX), 0)
    tall = iota((ROWS, TX), 0)
    deep = iota((Z, TX), 0)
    spread = iota((TY * TX, TX), 0)
    depth = CAP * TX
    for dy in (0, -1, 1):
        for n, dx in enumerate((-1, 0, 1)):
            values, cells = held(dx, dy)
            for k in range(CAP):
                cell = cells[k : k + 1, :]
                x = cell & (TX - 1)
                y = (cell >> 7) & (TY - 1)
                z = cell >> 10
                at = pl.ds(n * depth + k * TX, TX)
                if dy == 0:
                    hot[:, at] = ones(tall == cell >> 7)
                else:
                    z = jnp.where(y == (TY - 1 if dy < 0 else 0), z, -1)
                    levels[:, at] = ones(deep == z)
                parts = split(values[k], SPLIT)
                column = j == ((x + HALO) & (TX - 1))
                for side in range(2):
                    if dx == (1 if side == 0 else -1):
                        continue
                    inner = (dx == 0) == (side == 0)
                    use = column & ((j >= HALO) if inner else (j < HALO))
                    to = pl.ds((n - side) * depth + k * TX, TX)
                    for m in range(SPLIT):
                        for s in range(0, SRC, 2):
                            two = [jnp.where(use, parts[m][i : i + 1, :], 0.0) for i in (s, s + 1)]
                            near[side, m, 8 * s : 8 * s + 16, to] = cat(two).astype(BF16)
                if dx == 0:
                    to = pl.ds(k * TX, TX)
                    mask = deep == z
                    for m in range(SPLIT):
                        for s in range(SRC):
                            one = jnp.where(mask, parts[m][s : s + 1, :], 0.0)
                            wide[m, s * Z : (s + 1) * Z, to] = one.astype(BF16)
                    if dy == 0:
                        spots[:, to] = ones(spread == (cell & (TY * TX - 1)))
                    else:
                        spots[0:TX, to] = ones(iota((TX, TX), 0) == x)
        onehot = hot[...] if dy == 0 else levels[...]
        halves = []
        for side in range(2):
            some = onehot[:, side * depth : (side + 2) * depth]
            halves.append(sum(dot(some, near[side, m]) for m in range(SPLIT)))
        strip = jnp.concatenate(halves, axis=1)
        if dy == 0:
            strip_ref[...] = strip
            for y in range(0, TY, 2):
                some = spots[y * TX : (y + 2) * TX, :]
                got = sum(dot(wide[m], some) for m in range(SPLIT))
                for i in range(2):
                    for s in range(SRC):
                        main_ref[s, pl.ds(y + i, Z, stride=TY), :] = got[
                            s * Z : (s + 1) * Z, i * TX : (i + 1) * TX
                        ]
        else:
            side = 0 if dy < 0 else 1
            row_ref[side, SRC] = strip
            got = sum(dot(wide[m], spots[0:TX, :]) for m in range(SPLIT))
            for s in range(SRC):
                row_ref[side, s] = got[s * Z : (s + 1) * Z, :]


def core_kernel(
    rec_hbm, t_hbm, a_hbm, f_hbm, strip_hbm, y0_hbm, y1_hbm, h0_hbm, h1_hbm,
    last_ref, e0_ref, e1_ref, edge_ref, beyond_ref,
    rec_ref, t_ref, a_ref, f_ref, strip_in, y0_ref, y1_ref, h0_ref, h1_ref, strip_flags,
    turned, hot, levels, near, wide, spots, rows, flags, both, both_flags,
    g_ref, halo, back, adj, adj2, sems,
):
    pairs = (
        (rec_hbm, rec_ref),
        (y0_hbm, y0_ref),
        (y1_hbm, y1_ref),
        (strip_hbm, strip_in),
        (h0_hbm, h0_ref),
        (h1_hbm, h1_ref),
        (t_hbm, t_ref),
        (f_hbm, f_ref),
        (a_hbm, a_ref),
    )
    coming = [pltpu.make_async_copy(hbm, ref, sems.at[n]) for n, (hbm, ref) in enumerate(pairs)]
    all_start(coming)
    coming[0].wait()
    scatter(rec_ref, last_ref, last_ref.at[SRC], halo, turned, hot, levels, near, wide, spots)
    all_wait(coming[1:6])

    blank = jnp.zeros((PAD, TX), F32)
    for p in range(PLANES):
        for k in range(5):
            if p == SRC:
                take_rows(h0_ref[k], h1_ref[k], rows, flags, p, k)
            else:
                take_rows(y0_ref[k, p], y1_ref[k, p], rows, flags, p, k)
        for side in range(2):
            for k in (0, 2):
                rows[side, k, p, 0:PAD, :] = blank
                rows[side, k, p, PAD + Z : PAD + Z + PAD, :] = blank
    strip_flags[...] = strip_in[2].astype(I32)
    both[0] = both_sides(strip_in[0])
    both[1] = both_sides(strip_in[1])
    both_flags[...] = both_sides(strip_flags[...])
    lane = iota((TY, TX), 1)
    row = iota((TY, TX), 0)
    all_wait(coming[6:])

    def refs(p):
        if p < SRC:
            return t_ref.at[p], a_ref.at[p], f_ref.at[p]
        return strip_in.at[0], strip_in.at[1], strip_flags

    def at_level(z, carry):
        here = level(z)
        pair = [both[0, here, :], both[1, here, :], both_flags[here, :]]
        for p in range(PLANES):
            sides = [patch_of(v, p) for v in pair]
            shares, rden, total = shares_at(z, p, refs(p), sides, rows, flags, lane, row)
            for k, g in enumerate(shares):
                g_ref[k, p, here, :] = g
            source = last_ref[p, here, :] * rden
            last_ref[p, here, :] = source
            adj[p, here, :] = total + source
        return carry

    lax.fori_loop(0, Z, at_level, 0, unroll=2)

    wide_lane = iota((Z, TX), 1)
    for side in range(2):
        edge = pl.ds(0 if side == 0 else TY - 1, Z, stride=TY)
        here = pl.ds(PAD, Z)
        pair = [
            both_sides(rows[side, 0, SRC, here, :]),
            both_sides(rows[side, 2, SRC, here, :]),
            both_sides(flags[side, SRC, here, :]),
        ]
        for p in range(PLANES):
            t_p, a_p, f_p = refs(p)
            edge_ref[side, p] = g_ref[2 + side, p, edge, :]

            def at(k, shift=0):
                return rows[side, k, p, PAD + shift : PAD + shift + Z, :]

            t, a, f = at(0), at(2), flags[side, p, here, :]
            t2, a2 = at(3), at(4)
            t0, f0, a0 = t_p[edge, :], f_p[edge, :], a_p[edge, :]
            tl, tr = beside(t, patch_of(pair[0], p), wide_lane)
            al, ar = beside(a, patch_of(pair[1], p), wide_lane)
            fl, fr = beside(f, patch_of(pair[2], p), wide_lane)
            tm, tp = at(0, -1), at(0, 1)
            fm = flags[side, p, PAD - 1 : PAD - 1 + Z, :]
            fp = flags[side, p, PAD + 1 : PAD + 1 + Z, :]
            low, high = (t2, t0) if side == 0 else (t0, t2)
            den = 1.0 + coef(f, 1, tl, tr, t) + coef(f, 2, low, high, t) + coef(f, 4, tm, tp, t)
            rden = 1.0 / den
            inward = (given_high if side == 0 else given_low)(f0, 2, t0, t)
            total = halo[side, p] + given_low(fl, 1, tl, t) * al
            total = total + given_high(fr, 1, tr, t) * ar
            total = total + given_low(fm, 4, tm, t) * at(2, -1)
            total = total + given_high(fp, 4, tp, t) * at(2, 1)
            total = total + jnp.maximum(t2 - t, 0.0) * a2 + inward * a0
            halo[side, p] = total * rden
            back[side, p] = inward * rden

    def sweep(old, new, with_halo):
        both[0] = both_sides(old[SRC])

        def at_level(z, carry):
            here = level(z)
            below = level(jnp.maximum(z - 1, 0))
            above = level(jnp.minimum(z + 1, Z - 1))
            sides = both[0, here, :]
            for p in range(PLANES):
                v = old[p, here, :]
                left, right = beside(v, patch_of(sides, p), lane)
                low, high = 0.0, 0.0
                if with_halo:
                    low = jnp.broadcast_to(halo[0, p, pl.ds(z, 1), :], (TY, TX))
                    high = jnp.broadcast_to(halo[1, p, pl.ds(z, 1), :], (TY, TX))
                down = jnp.where(row == 0, low, pltpu.roll(v, 1, 0))
                up = jnp.where(row == TY - 1, high, pltpu.roll(v, TY - 1, 0))
                total = last_ref[p, here, :]
                for k, w in enumerate((left, right, down, up, old[p, below, :], old[p, above, :])):
                    total = total + g_ref[k, p, here, :] * w
                new[p, here, :] = total
            return carry

        lax.fori_loop(0, Z, at_level, 0, unroll=4)

    sweep(adj, adj2, True)
    sweep(adj2, last_ref, False)

    low, high = pl.ds(0, Z, stride=TY), pl.ds(TY - 1, Z, stride=TY)

    def pack(out, up):
        edge = high if up else low
        total = None
        for p in range(PLANES):
            out[p] = adj2[p, edge, :]
            if p < SRC:
                part = last_ref[p, edge, :]
                total = part if total is None else total + part
        out[PLANES] = total

    by_parity("gy", e0_ref, e1_ref, pack)
    for side, edge in enumerate((low, high)):
        total = None
        for s in range(SRC):
            part = back[side, s] * adj2[s, edge, :]
            total = part if total is None else total + part
        beyond_ref[side] = total


def gradient_kernel(
    last_ref, y0_ref, y1_ref, edge_ref, beyond_ref, slow_ref, adj_ref, grad_ref, fix, above, patch
):
    even_y = is_even("gy")
    for p in range(PLANES + 1):
        first, second = y0_ref[p], y1_ref[p]
        from_low = jnp.where(even_y, second, first)
        from_high = jnp.where(even_y, first, second)
        if p < PLANES:
            fix[0, p] = edge_ref[0, p] * from_low
            fix[1, p] = edge_ref[1, p] * from_high
        else:
            above[0] = beyond_ref[0] + from_low
            above[1] = beyond_ref[1] + from_high
    lane = iota((TY, TX), 1)
    row = iota((TY, TX), 0)

    def wide(ref, z, *index):
        return jnp.broadcast_to(ref[(*index, pl.ds(z, 1), slice(None))], (TY, TX))

    def completed(z, p):
        low, high = wide(fix, z, 0, p), wide(fix, z, 1, p)
        return last_ref[p, level(z), :] + jnp.where(
            row == 0, low, jnp.where(row == TY - 1, high, 0.0)
        )

    def strip_level(z, carry):
        patch[level(z), :] = completed(z, SRC)
        return carry

    lax.fori_loop(0, Z, strip_level, 0, unroll=8)
    strip = patch[...]
    for by in (8, 16, 32):
        strip = strip + turn(strip, by)
    patch[...] = jnp.where(iota((ROWS, TX), 1) == 0, turn(strip, -59), turn(strip, 3))

    def at_level(z, carry):
        here = level(z)
        total = None
        for p in range(SRC):
            v = completed(z, p)
            adj_ref[p, here, :] = v
            total = v if total is None else total + v
        left, right = beside(total, patch[here, :], lane)
        down = jnp.where(row == 0, wide(above, z, 0), pltpu.roll(total, 1, 0))
        up = jnp.where(row == TY - 1, wide(above, z, 1), pltpu.roll(total, TY - 1, 0))
        beside_it = right + left + up + down
        grad_ref[here, :] = slow_ref[here, :] * (total + 0.125 * (beside_it - 4.0 * total))
        return carry

    lax.fori_loop(0, Z, at_level, 0, unroll=4)


def f32(*shape):
    return jax.ShapeDtypeStruct(shape, F32)


def call(kernel, outs, scratch, flops, ins=(), outs_in=(), limit=20):
    vmem = pl.BlockSpec(memory_space=pltpu.VMEM)

    def run(*args):
        moved = sum(a.size * 4 for a in args)
        given = [pl.BlockSpec(memory_space=s) for s in ins]
        kept = [pl.BlockSpec(memory_space=s) for s in outs_in]
        return pl.pallas_call(
            kernel,
            out_shape=outs,
            in_specs=given + [vmem] * (len(args) - len(given)),
            out_specs=kept + [vmem] * (len(outs) - len(kept)),
            scratch_shapes=scratch,
            compiler_params=pltpu.CompilerParams(vmem_limit_bytes=limit << 20),
            cost_estimate=pl.CostEstimate(flops=flops, bytes_accessed=moved, transcendentals=0),
        )(*args)

    return run


def swapped(v, axis, count, odd):
    pairs = [(i, i + 1) for i in range(odd, count - 1, 2)]
    return lax.ppermute(v, axis, [(a, b) for a, b in pairs] + [(b, a) for a, b in pairs])


def shards(traveltime, adjoint_start, upwind_flags, slowness, residual_rows, station_tile, station_cell):
    devices = lax.axis_size(("gx", "gy"))
    nx, ny = lax.axis_size("gx"), lax.axis_size("gy")
    count = residual_rows.shape[0]
    t, a, f = (v.reshape(SRC, ROWS, TX) for v in (traveltime, adjoint_start, upwind_flags))
    whole = (SRC, ROWS, TX)

    x_out0, x_out1, y_out0, y_out1, own = call(
        leaving_kernel,
        [
            f32(ROWS, TX),
            f32(ROWS, TX),
            f32(5, SRC, Z, TX),
            f32(5, SRC, Z, TX),
            f32(3, ROWS, TX),
        ],
        [
            pltpu.VMEM(whole, F32),
            pltpu.VMEM(whole, F32),
            pltpu.VMEM(whole, I32),
            pltpu.SemaphoreType.DMA((3, ROWS // PART)),
        ],
        10**6,
        ins=[pltpu.HBM] * 3,
        limit=LEAVING_LIMIT,
    )(t, a, f)
    x_in0 = swapped(x_out0, "gx", nx, 0)
    x_in1 = swapped(x_out1, "gx", nx, 1)
    y_in0 = swapped(y_out0, "gy", ny, 0)
    y_in1 = swapped(y_out1, "gy", ny, 1)
    (sent,) = call(
        records_kernel,
        [f32(devices * 3, TX)],
        [
            pltpu.VMEM((SRC, count), F32),
            pltpu.VMEM((1, count), I32),
            pltpu.VMEM((1, count), I32),
            pltpu.VMEM((3, GROUP, count), F32),
            pltpu.VMEM((devices + 64, TX), F32),
            pltpu.SemaphoreType.DMA((3,)),
        ],
        10**6,
        ins=[pltpu.HBM] * 3,
        limit=RECORDS_LIMIT,
    )(residual_rows.T, station_tile.reshape(1, count), station_cell.reshape(1, count))
    got = lax.all_to_all(sent.reshape(devices, 1, 3 * TX), ("gx", "gy"), 0, 0, tiled=True)
    got = got.reshape(devices * 3, TX)

    strip, h_out0, h_out1 = call(
        strips_kernel,
        [f32(3, ROWS, TX), f32(5, Z, TX), f32(5, Z, TX)],
        [
            pltpu.VMEM((3, ROWS, TX), F32),
            pltpu.VMEM((ROWS, TX), I32),
            pltpu.SemaphoreType.DMA((1,)),
        ],
        10**6,
        outs_in=[pltpu.HBM],
    )(own, x_in0, x_in1)
    h_in0 = swapped(h_out0, "gy", ny, 0)
    h_in1 = swapped(h_out1, "gy", ny, 1)

    depth = CAP * TX
    last, e_out0, e_out1, edges, beyond = call(
        core_kernel,
        [
            f32(PLANES, ROWS, TX),
            f32(PLANES + 1, Z, TX),
            f32(PLANES + 1, Z, TX),
            f32(2, PLANES, Z, TX),
            f32(2, Z, TX),
        ],
        [
            pltpu.VMEM((devices * 3, TX), F32),
            pltpu.VMEM(whole, F32),
            pltpu.VMEM(whole, F32),
            pltpu.VMEM(whole, I32),
            pltpu.VMEM((3, ROWS, TX), F32),
            pltpu.VMEM((5, SRC, Z, TX), F32),
            pltpu.VMEM((5, SRC, Z, TX), F32),
            pltpu.VMEM((5, Z, TX), F32),
            pltpu.VMEM((5, Z, TX), F32),
            pltpu.VMEM((ROWS, TX), I32),
            pltpu.VMEM((3, TX, TX), F32),
            pltpu.VMEM((ROWS, 3 * depth), BF16),
            pltpu.VMEM((Z, 3 * depth), BF16),
            pltpu.VMEM((2, SPLIT, SRC * 8, 2 * depth), BF16),
            pltpu.VMEM((SPLIT, SRC * Z, depth), BF16),
            pltpu.VMEM((TY * TX, depth), BF16),
            pltpu.VMEM((2, 5, PLANES, Z + 2 * PAD, TX), F32),
            pltpu.VMEM((2, PLANES, Z + 2 * PAD, TX), I32),
            pltpu.VMEM((2, ROWS, TX), F32),
            pltpu.VMEM((ROWS, TX), I32),
            pltpu.VMEM((6, PLANES, ROWS, TX), F32),
            pltpu.VMEM((2, PLANES, Z, TX), F32),
            pltpu.VMEM((2, PLANES, Z, TX), F32),
            pltpu.VMEM((PLANES, ROWS, TX), F32),
            pltpu.VMEM((PLANES, ROWS, TX), F32),
            pltpu.SemaphoreType.DMA((9,)),
        ],
        10**8,
        ins=[pltpu.HBM] * 9,
        limit=CORE_LIMIT,
    )(got, t, a, f, strip, y_in0, y_in1, h_in0, h_in1)
    e_in0 = swapped(e_out0, "gy", ny, 0)
    e_in1 = swapped(e_out1, "gy", ny, 1)

    adjoint, gradient = call(
        gradient_kernel,
        [f32(*whole), f32(ROWS, TX)],
        [
            pltpu.VMEM((2, PLANES, Z, TX), F32),
            pltpu.VMEM((2, Z, TX), F32),
            pltpu.VMEM((ROWS, TX), F32),
        ],
        10**6,
    )(last, e_in0, e_in1, edges, beyond, slowness.reshape(ROWS, TX))
    return adjoint.reshape(traveltime.shape), gradient.reshape(slowness.shape)


def solution(mesh):
    placed = (
        P(None, None, "gy", "gx"),
        P(None, None, "gy", "gx"),
        P(None, None, "gy", "gx"),
        P(None, "gy", "gx"),
        P(("gx", "gy"), None),
        P(("gx", "gy"), None),
        P(("gx", "gy")),
    )

    return jax.shard_map(
        shards,
        mesh=mesh,
        in_specs=placed,
        out_specs=(P(None, None, "gy", "gx"), P(None, "gy", "gx")),
        check_vma=False,
    )
```

time: 88 us -> 69.7 us (0.79)
  blocking collectives: 19.5 us -> 0 us
  Pallas kernels: 38 us -> 23.3 us
  starting transfers between devices: 13.2 us -> 26.1 us
  waiting for transfers between devices: 12.2 us -> 17.8 us
  local copies, waits for them, and re-layouts: 3.91 us -> 1.27 us
    all_to_all x1 -> x0, blocking collectives: 19.5 us -> none  [shards(): got = lax.all_to_all(sent, ('gx', 'gy'), 0, 0, tiled=True)]
    pallas_call x6 -> x5, Pallas kernels: 38 us -> 23.3 us  [run(): pl.pallas_call(kernel, out_shape=outs, in_specs=given + [vmem] * (len(arg...]
    all_to_all x0 -> x1, starting transfers between devices: none -> 10.5 us  [shards(): lax.all_to_all(sent.reshape(devices, 1, 3 * TX), ('gx', 'gy'), 0, 0, tile...]
    ppermute x6 -> x8, waiting for transfers between devices: 12.2 us -> 17.8 us  [swapped(): lax.ppermute(v, axis, [(a, b) for a, b in pairs] + [(b, a) for a, b in pa...]
    unnamed x17 -> x4, local copies, waits for them, and re-layouts: 3.71 us -> 1.27 us
    ppermute x6 -> x8, starting transfers between devices: 13.2 us -> 15.6 us  [swapped(): lax.ppermute(v, axis, [(a, b) for a, b in pairs] + [(b, a) for a, b in pa...]
  transfers between devices with their start and end apart: 6 -> 9, of which waited for: 3 -> 3; matrix products, arithmetic and copies ran while one was open for 0% -> 0% of each run, Pallas kernels for 1% -> 4%
where the time goes in v1:
time: 69.7 us; the launch traced here: 69.2 us
  starting transfers between devices  26.1 us (37%)
  Pallas kernels  23.3 us (33%)
  waiting for transfers between devices  17.8 us (26%)
  local copies, waits for them, and re-layouts  1.27 us (2%)
  between operations  0.74 us (1%)
    pallas_call x5, Pallas kernels, run(): pl.pallas_call(kernel, out_shape=outs, in_specs=given + [vmem] * (len(arg...  23.3 us
    ppermute x8, waiting for transfers between devices, swapped(): lax.ppermute(v, axis, [(a, b) for a, b in pairs] + [(b, a) for a, b in pa...  17.8 us
    ppermute x8, starting transfers between devices, swapped(): lax.ppermute(v, axis, [(a, b) for a, b in pairs] + [(b, a) for a, b in pa...  15.6 us
    all_to_all x1, starting transfers between devices, shards(): lax.all_to_all(sent.reshape(devices, 1, 3 * TX), ('gx', 'gy'), 0, 0, tile...  10.5 us
  transfers between devices with their start and end apart: 9, of which 3 were waited for; matrix products, arithmetic and copies ran while one was open for 0% of the time, Pallas kernels for 4%

profile of v1, /device:TPU:23, one launch (start us, length us, event | category | flops | bytes accessed | tf_op | source)
XLA Modules:
  0.0 69.2 jit_solution(12898512000468865867)
XLA Ops:
  0.6 4.7 %shard_map.87 = (f32[256,128]{1,0:T(8,128)S(1)}, f32[256,128]{1,0:T(8,128)S(1)}, f32[5,8,32,128]{3,2,1,0:T(8,128)}, f32[5,8,32,128]{3,2,1,0:T(8,128)S(1)}, f32[3,256,128]{2,1,0:T(8,128)S(1)}) custom-call(f32[8,256,128]{2,1,0:T(8,128)} %bitcast.13, f32[8,256,128]{2,1,0:T(8,128)} %bitcast.15, s32[8,256,128]{2,1,0:T(8,128)} %bitcast.17), custom_call_target="tpu_custom_call" | custom-call | flops 1000000 | bytes 3145728 | tf_op jit(solution)/shard_map/pallas_call | solution.py:596
  5.4 0.7 %collective-permute-start.2 = (f32[5,8,32,128]{3,2,1,0:T(8,128)}, f32[5,8,32,128]{3,2,1,0:T(8,128)S(1)}, u32[]{:S(2)}, u32[]{:S(2)}) collective-permute-start(f32[5,8,32,128]{3,2,1,0:T(8,128)} %get-tuple-element.21), channel_id=1, source_target_pairs={{0,1},{2,3},{4,5},{6,7},{8,9},{10,11},{12,13},{14,15},{1,0},{3,2},... | collective-permute-start | bytes 1966088 | tf_op jit(solution)/shard_map/ppermute | solution.py:611
  6.1 3.4 %collective-permute-start.3 = (f32[5,8,32,128]{3,2,1,0:T(8,128)S(1)}, f32[5,8,32,128]{3,2,1,0:T(8,128)S(1)}, u32[]{:S(2)}, u32[]{:S(2)}) collective-permute-start(f32[5,8,32,128]{3,2,1,0:T(8,128)S(1)} %get-tuple-element.22), channel_id=1, source_target_pairs={{1,2},{3,4},{5,6},{7,8},{9,10},{11,12},{13,14},{2,1},{4,3},{6,5},{... | collective-permute-start | bytes 1966088 | tf_op jit(solution)/shard_map/ppermute | solution.py:611
  9.6 3.4 %collective-permute-start = (f32[256,128]{1,0:T(8,128)S(1)}, f32[256,128]{1,0:T(8,128)S(1)}, u32[]{:S(2)}, u32[]{:S(2)}) collective-permute-start(f32[256,128]{1,0:T(8,128)S(1)} %get-tuple-element.18), channel_id=1, source_target_pairs={{0,16},{32,48},{64,80},{96,112},{16,0},{48,32},{80,64},{112,96},{1... | collective-permute-start | bytes 393224 | tf_op jit(solution)/shard_map/ppermute | solution.py:611
  12.9 2.2 %collective-permute-start.1 = (f32[256,128]{1,0:T(8,128)S(1)}, f32[256,128]{1,0:T(8,128)S(1)}, u32[]{:S(2)}, u32[]{:S(2)}) collective-permute-start(f32[256,128]{1,0:T(8,128)S(1)} %get-tuple-element.19), channel_id=1, source_target_pairs={{16,32},{48,64},{80,96},{32,16},{64,48},{96,80},{17,33},{49,65},{8... | collective-permute-start | bytes 393224 | tf_op jit(solution)/shard_map/ppermute | solution.py:611
  15.1 2.0 %shard_map.86 = f32[384,128]{1,0:T(8,128)} custom-call(f32[8,256]{1,0:T(8,128)} %bitcast.20, s32[1,256]{1,0:T(1,128)} %bitcast.21, s32[1,256]{1,0:T(1,128)} %bitcast.22), custom_call_target="tpu_custom_call" | custom-call | flops 1000000 | bytes 10240 | tf_op jit(solution)/shard_map/pallas_call | solution.py:596
  17.1 10.5 %all-to-all-start = ((f32[128,1,384]{2,1,0:T(1,128)}), f32[128,1,384]{2,1,0:T(1,128)S(1)}, u32[]{:S(2)}, u32[]{:S(2)}) async-start(f32[128,1,384]{2,1,0:T(1,128)} %bitcast.19), calls=%async_computation | async-start | bytes 393216 | tf_op jit(solution)/shard_map/all_to_all | solution.py:659
  27.6 7.9 %collective-permute-done.x0_ref = f32[256,128]{1,0:T(8,128)S(1)} collective-permute-done((f32[256,128]{1,0:T(8,128)S(1)}, f32[256,128]{1,0:T(8,128)S(1)}, u32[]{:S(2)}, u32[]{:S(2)}) %collective-permute-start) | collective-permute-done | bytes 131104 | tf_op jit(solution)/shard_map/ppermute | solution.py:611
  35.5 0.0 collective-permute-done.1.x1_ref
  35.5 0.5 shard_map.88
  36.1 0.1 collective-permute-start.4
  36.2 2.6 %collective-permute-start.5 = (f32[5,32,128]{2,1,0:T(8,128)S(1)}, f32[5,32,128]{2,1,0:T(8,128)S(1)}, u32[]{:S(2)}, u32[]{:S(2)}) collective-permute-start(f32[5,32,128]{2,1,0:T(8,128)S(1)} %get-tuple-element.24), channel_id=1, source_target_pairs={{1,2},{3,4},{5,6},{7,8},{9,10},{11,12},{13,14},{2,1},{4,3},{6,5},{... | collective-permute-start | bytes 245768 | tf_op jit(solution)/shard_map/ppermute | solution.py:611
  38.8 0.0 all-to-all-done
  38.8 0.0 collective-permute-done.4.h0_hbm
  38.8 4.1 %collective-permute-done.5.h1_hbm = f32[5,32,128]{2,1,0:T(8,128)S(1)} collective-permute-done((f32[5,32,128]{2,1,0:T(8,128)S(1)}, f32[5,32,128]{2,1,0:T(8,128)S(1)}, u32[]{:S(2)}, u32[]{:S(2)}) %collective-permute-start.5) | collective-permute-done | bytes 81952 | tf_op jit(solution)/shard_map/ppermute | solution.py:611
  42.9 0.0 collective-permute-done.2.y0_hbm
  42.9 0.0 collective-permute-done.3.y1_hbm
  42.9 0.0 copy-start.1
  42.9 13.8 %shard_map.89 = (f32[9,256,128]{2,1,0:T(8,128)}, f32[10,32,128]{2,1,0:T(8,128)S(1)}, f32[10,32,128]{2,1,0:T(8,128)S(1)}, f32[2,9,32,128]{3,2,1,0:T(8,128)S(1)}, f32[2,32,128]{2,1,0:T(8,128)S(1)}) custom-call(f32[384,128]{1,0:T(8,128)S(1)} %bitcast.11, f32[8,256,128]{2,1,0:T(8,128)} %bitcast.14, f32[8,256,128]{2,1,0:T(8,128)} %bitcast.16, ...), custom_call_target="tpu_custom_call" | custom-call | flops 100000000 | bytes 5210112 | tf_op jit(solution)/shard_map/pallas_call | solution.py:596
  56.8 0.6 collective-permute-start.6
  57.3 2.5 %collective-permute-start.7 = (f32[10,32,128]{2,1,0:T(8,128)S(1)}, f32[10,32,128]{2,1,0:T(8,128)S(1)}, u32[]{:S(2)}, u32[]{:S(2)}) collective-permute-start(f32[10,32,128]{2,1,0:T(8,128)S(1)} %get-tuple-element.27), channel_id=1, source_target_pairs={{1,2},{3,4},{5,6},{7,8},{9,10},{11,12},{13,14},{2,1},{4,3},{6,5},{... | collective-permute-start | bytes 491528 | tf_op jit(solution)/shard_map/ppermute | solution.py:611
  59.9 0.0 collective-permute-done.6.y0_ref
  59.9 5.8 %collective-permute-done.7.y1_ref = f32[10,32,128]{2,1,0:T(8,128)S(1)} collective-permute-done((f32[10,32,128]{2,1,0:T(8,128)S(1)}, f32[10,32,128]{2,1,0:T(8,128)S(1)}, u32[]{:S(2)}, u32[]{:S(2)}) %collective-permute-start.7) | collective-permute-done | bytes 163872 | tf_op jit(solution)/shard_map/ppermute | solution.py:611
  65.7 0.0 copy-done.1
  65.7 0.0 copy-start
  65.7 1.3 %copy-done = f32[9,256,128]{2,1,0:T(8,128)S(1)} copy-done((f32[9,256,128]{2,1,0:T(8,128)S(1)}, f32[9,256,128]{2,1,0:T(8,128)}, u32[]{:S(2)}) %copy-start) | copy-done | bytes 1179672
  67.0 2.2 %shard_map.90 = (f32[8,256,128]{2,1,0:T(8,128)}, f32[256,128]{1,0:T(8,128)}) custom-call(f32[9,256,128]{2,1,0:T(8,128)S(1)} %copy-done, f32[10,32,128]{2,1,0:T(8,128)S(1)} %collective-permute-done.6.y0_ref, f32[10,32,128]{2,1,0:T(8,128)S(1)} %collective-permute-done.7.y1_ref, f32[2,9,32,128]{3,2,1,0:T(8,128)S(1)} %get-tuple-element.28.edge_ref, ...), custom_call_target="tpu_custom_call" | custom-call | flops 1000000 | bytes 1966080 | tf_op jit(solution)/shard_map/pallas_call | solution.py:596
Async XLA Ops:
  5.4 37.5 %collective-permute-start.2 = (f32[5,8,32,128]{3,2,1,0:T(8,128)}, f32[5,8,32,128]{3,2,1,0:T(8,128)S(1)}, u32[]{:S(2)}, u32[]{:S(2)}) collective-permute-start(f32[5,8,32,128]{3,2,1,0:T(8,128)} %get-tuple-element.21), channel_id=1, source_target_pairs={{0,1},{2,3},{4,5},{6,7},{8,9},{10,11},{12,13},{14,15},{1,0},{3,2},... | collective-permute-start | bytes 1966088 | tf_op jit(solution)/shard_map/ppermute | solution.py:611
  6.1 36.8 %collective-permute-start.3 = (f32[5,8,32,128]{3,2,1,0:T(8,128)S(1)}, f32[5,8,32,128]{3,2,1,0:T(8,128)S(1)}, u32[]{:S(2)}, u32[]{:S(2)}) collective-permute-start(f32[5,8,32,128]{3,2,1,0:T(8,128)S(1)} %get-tuple-element.22), channel_id=1, source_target_pairs={{1,2},{3,4},{5,6},{7,8},{9,10},{11,12},{13,14},{2,1},{4,3},{6,5},{... | collective-permute-start | bytes 1966088 | tf_op jit(solution)/shard_map/ppermute | solution.py:611
  9.6 25.9 %collective-permute-start = (f32[256,128]{1,0:T(8,128)S(1)}, f32[256,128]{1,0:T(8,128)S(1)}, u32[]{:S(2)}, u32[]{:S(2)}) collective-permute-start(f32[256,128]{1,0:T(8,128)S(1)} %get-tuple-element.18), channel_id=1, source_target_pairs={{0,16},{32,48},{64,80},{96,112},{16,0},{48,32},{80,64},{112,96},{1... | collective-permute-start | bytes 393224 | tf_op jit(solution)/shard_map/ppermute | solution.py:611
  12.9 22.6 %collective-permute-start.1 = (f32[256,128]{1,0:T(8,128)S(1)}, f32[256,128]{1,0:T(8,128)S(1)}, u32[]{:S(2)}, u32[]{:S(2)}) collective-permute-start(f32[256,128]{1,0:T(8,128)S(1)} %get-tuple-element.19), channel_id=1, source_target_pairs={{16,32},{48,64},{80,96},{32,16},{64,48},{96,80},{17,33},{49,65},{8... | collective-permute-start | bytes 393224 | tf_op jit(solution)/shard_map/ppermute | solution.py:611
  17.1 21.7 %all-to-all-start = ((f32[128,1,384]{2,1,0:T(1,128)}), f32[128,1,384]{2,1,0:T(1,128)S(1)}, u32[]{:S(2)}, u32[]{:S(2)}) async-start(f32[128,1,384]{2,1,0:T(1,128)} %bitcast.19), calls=%async_computation | async-start | bytes 393216 | tf_op jit(solution)/shard_map/all_to_all | solution.py:659
  36.1 2.8 %collective-permute-start.4 = (f32[5,32,128]{2,1,0:T(8,128)S(1)}, f32[5,32,128]{2,1,0:T(8,128)S(1)}, u32[]{:S(2)}, u32[]{:S(2)}) collective-permute-start(f32[5,32,128]{2,1,0:T(8,128)S(1)} %get-tuple-element.23), channel_id=1, source_target_pairs={{0,1},{2,3},{4,5},{6,7},{8,9},{10,11},{12,13},{14,15},{1,0},{3,2},... | collective-permute-start | bytes 245768 | tf_op jit(solution)/shard_map/ppermute | solution.py:611
  36.2 6.7 %collective-permute-start.5 = (f32[5,32,128]{2,1,0:T(8,128)S(1)}, f32[5,32,128]{2,1,0:T(8,128)S(1)}, u32[]{:S(2)}, u32[]{:S(2)}) collective-permute-start(f32[5,32,128]{2,1,0:T(8,128)S(1)} %get-tuple-element.24), channel_id=1, source_target_pairs={{1,2},{3,4},{5,6},{7,8},{9,10},{11,12},{13,14},{2,1},{4,3},{6,5},{... | collective-permute-start | bytes 245768 | tf_op jit(solution)/shard_map/ppermute | solution.py:611
  42.9 22.8 %copy-start.1 = (f32[32,8,128]{2,1,0:T(8,128)S(1)}, f32[32,8,128]{2,1,0:T(8,128)}, u32[]{:S(2)}) copy-start(f32[32,8,128]{2,1,0:T(8,128)} %param.10) | copy-start | bytes 393220
  56.8 3.1 %collective-permute-start.6 = (f32[10,32,128]{2,1,0:T(8,128)S(1)}, f32[10,32,128]{2,1,0:T(8,128)S(1)}, u32[]{:S(2)}, u32[]{:S(2)}) collective-permute-start(f32[10,32,128]{2,1,0:T(8,128)S(1)} %get-tuple-element.26), channel_id=1, source_target_pairs={{0,1},{2,3},{4,5},{6,7},{8,9},{10,11},{12,13},{14,15},{1,0},{3,2},... | collective-permute-start | bytes 491528 | tf_op jit(solution)/shard_map/ppermute | solution.py:611
  57.3 8.4 %collective-permute-start.7 = (f32[10,32,128]{2,1,0:T(8,128)S(1)}, f32[10,32,128]{2,1,0:T(8,128)S(1)}, u32[]{:S(2)}, u32[]{:S(2)}) collective-permute-start(f32[10,32,128]{2,1,0:T(8,128)S(1)} %get-tuple-element.27), channel_id=1, source_target_pairs={{1,2},{3,4},{5,6},{7,8},{9,10},{11,12},{13,14},{2,1},{4,3},{6,5},{... | collective-permute-start | bytes 491528 | tf_op jit(solution)/shard_map/ppermute | solution.py:611
  65.7 1.3 %copy-start = (f32[9,256,128]{2,1,0:T(8,128)S(1)}, f32[9,256,128]{2,1,0:T(8,128)}, u32[]{:S(2)}) copy-start(f32[9,256,128]{2,1,0:T(8,128)} %get-tuple-element.25.last_ref) | copy-start | bytes 3538948
